TPU v7x, 256 devices: a whole 4x4x8 slice. The times are simulated.
256 devices in a mesh: rep: 1, dp: 256 (over x, y, z, core).
Axes of the slice: x: 4, y: 4, z: 8, core: 2. Of those that a mesh axis runs over, the one named last changes fastest.
Arguments:
- x: bfloat16 [256, 1024, 1024], P(('rep', 'dp'))
- dy: bfloat16 [256, 1024, 1024], P(('rep', 'dp'))
- w_gate: bfloat16 [2, 1024, 4096], P(None, 'dp')
- w_up: bfloat16 [2, 1024, 4096], P(None, 'dp')
- w_down: bfloat16 [2, 4096, 1024], P(None, 'dp')
Outputs:
- output 1: bfloat16 [256, 1024, 1024], P(('rep', 'dp'))
- output 2: bfloat16 [2, 1024, 4096], P('rep', 'dp')
- output 3: bfloat16 [2, 1024, 4096], P('rep', 'dp')
- output 4: bfloat16 [2, 4096, 1024], P('rep', 'dp')
All inputs are finite; a program needn't handle non-finite values.
Results may differ from a plain program's by a relative error of at most 0.018.
Values are sent between devices in bfloat16 or wider.
A program may use at most 768 MiB of HBM per device.

v0:
```python
import jax
import jax.numpy as jnp
from jax import lax

NAMES = ("w_gate", "w_up", "w_down")


def matmul(a, w):
    return jnp.dot(a, w, preferred_element_type=jnp.float32).astype(jnp.bfloat16)


def normed(h):
    wide = h.astype(jnp.float32)
    scale = lax.rsqrt(jnp.mean(wide**2, -1, keepdims=True) + 1e-6)
    return (wide * scale).astype(jnp.bfloat16)


def layer(h, w):
    a = normed(h)
    gate = jnp.dot(a, w["w_gate"], preferred_element_type=jnp.float32)
    up = jnp.dot(a, w["w_up"], preferred_element_type=jnp.float32)
    return h + matmul((jax.nn.silu(gate) * up).astype(jnp.bfloat16), w["w_down"])


def stack(weights, h):
    for number in range(weights["w_gate"].shape[0]):
        h = layer(h, {name: w[number] for name, w in weights.items()})
    return h


def solution(mesh):
    groups = mesh.shape["rep"]

    def step(x, dy, *weights):
        shape = x.shape
        x, dy = (t.reshape(groups, -1, *t.shape[1:]) for t in (x, dy))

        def of_a_group(x, dy):
            _, back = jax.vjp(stack, dict(zip(NAMES, weights, strict=True)), x)
            by_weights, by_x = back(dy)
            return (by_x, *(by_weights[name] for name in NAMES))

        by_x, *by_weights = jax.vmap(of_a_group)(x, dy)
        return (by_x.reshape(shape), *(t.reshape(-1, *t.shape[2:]) for t in by_weights))

    return step
```

profile of v0, /device:TPU:1, one launch (start us, length us, event | category | flops | bytes accessed | tf_op | source)
XLA Modules:
  0.0 3507.5 jit_solution(920574095465774584)
XLA Ops:
  22.0 119.5 %all-gather.29.cloned.1.call-done = bf16[1,1024,4096]{2,0,1:T(2,128)(2,1)} async-done(((bf16[1,4,4096]{2,0,1:T(2,128)(2,1)}), bf16[1,1024,4096]{2,0,1:T(2,128)(2,1)}) %all-gather.29.cloned.1.call-update) | async-done | bytes 8388624 | tf_op jit(solution)/vmap(jvp())/squeeze | solution.py:27
  141.5 17.4 fusion.40
  158.9 109.2 %all-gather.31.cloned.1.call-done = bf16[1,1024,4096]{2,0,1:T(2,128)(2,1)} async-done(((bf16[1,4,4096]{2,0,1:T(2,128)(2,1)}), bf16[1,1024,4096]{2,0,1:T(2,128)(2,1)}) %all-gather.31.cloned.1.call-update) | async-done | bytes 8388624 | tf_op jit(solution)/vmap(jvp())/squeeze | solution.py:27
  268.2 17.7 fusion.36
  300.7 86.4 %all-gather.33.cloned.1.call-done = bf16[1,4096,1024]{2,1,0:T(8,128)(2,1)} async-done(((bf16[1,16,1024]{2,1,0:T(8,128)(2,1)}), bf16[1,4096,1024]{2,1,0:T(8,128)(2,1)}) %all-gather.33.cloned.1.call-update) | async-done | bytes 8388624 | tf_op jit(solution)/vmap(jvp())/squeeze | solution.py:27
  387.1 14.9 fusion.65
  402.1 111.2 %all-gather.35.cloned.1.call-done = bf16[1,1024,4096]{2,0,1:T(2,128)(2,1)} async-done(((bf16[1,4,4096]{2,0,1:T(2,128)(2,1)}), bf16[1,1024,4096]{2,0,1:T(2,128)(2,1)}) %all-gather.35.cloned.1.call-update) | async-done | bytes 8388624 | tf_op jit(solution)/vmap(jvp())/squeeze | solution.py:27
  513.3 18.4 fusion.33
  531.7 100.4 %all-gather.37.cloned.1.call-done = bf16[1,4096,1024]{2,1,0:T(8,128)(2,1)} async-done(((bf16[1,16,1024]{2,1,0:T(8,128)(2,1)}), bf16[1,4096,1024]{2,1,0:T(8,128)(2,1)}) %all-gather.37.cloned.1.call-update) | async-done | bytes 8388624 | tf_op jit(solution)/vmap(jvp())/squeeze | solution.py:27
  646.9 110.8 %all-gather.39.cloned.1.call-done = bf16[1,1024,4096]{2,0,1:T(2,128)(2,1)} async-done(((bf16[1,4,4096]{2,0,1:T(2,128)(2,1)}), bf16[1,1024,4096]{2,0,1:T(2,128)(2,1)}) %all-gather.39.cloned.1.call-update) | async-done | bytes 8388624 | tf_op jit(solution)/vmap(jvp())/squeeze | solution.py:27
  757.7 17.4 fusion.28
  775.1 50.5 %fusion.31 = bf16[1024,1024]{0,1:T(8,128)(2,1)} fusion(bf16[1,1024,4096]{2,0,1:T(2,128)(2,1)} %all-gather.35.cloned.1.call-done, f32[1024,4096]{1,0:T(8,128)} %fusion.33, f32[1024,4096]{1,0:T(8,128)} %fusion.28, bf16[1024,4096]{1,0:T(8,128)(2,1)} %fusion.55), kind=kOutput, calls=%fused_computation.40 | convolution fusion | flops 8636071936 | bytes 52428800 | tf_op jit(solution)/vmap(transpose(jvp()))/dot_general | solution.py:20
  825.7 48.3 %fusion.67 = (f32[1024]{0:T(1024)S(1)}, bf16[1024,1024]{0,1:T(8,128)(2,1)}) fusion(bf16[1,1024,1024]{1,2,0:T(8,128)(2,1)S(1)} %copy-done.3, bf16[1024,1024]{0,1:T(8,128)(2,1)} %fusion.31, bf16[1,1024,4096]{2,0,1:T(2,128)(2,1)} %all-gather.39.cloned.1.call-done, bf16[1024,4096]{1,0:T(8,128)(2,1)} %fusion.55, f32[1024,4096]{1,0:T(8,128)} %fusion.33), kind=kOutput, calls=%fused_computation.82 | convolution fusion | flops 8621390848 | bytes 39849984 | tf_op jit(solution)/vmap(transpose(jvp()))/dot_general | solution.py:21
  878.4 15.3 fusion.80
  893.8 19.5 fusion.26
  927.9 51.0 %fusion.38 = bf16[1024,1024]{0,1:T(8,128)(2,1)} fusion(bf16[1,1024,4096]{2,0,1:T(2,128)(2,1)} %all-gather.29.cloned.1.call-done, f32[1024,4096]{1,0:T(8,128)} %fusion.40, f32[1024,4096]{1,0:T(8,128)} %fusion.36, bf16[1024,4096]{1,0:T(8,128)(2,1)} %fusion.52), kind=kOutput, calls=%fused_computation.47 | convolution fusion | flops 8636071936 | bytes 52428800 | tf_op jit(solution)/vmap(transpose(jvp()))/dot_general | solution.py:20
  978.9 48.1 %fusion.64 = (f32[1024]{0:T(1024)S(1)}, bf16[1024,1024]{0,1:T(8,128)(2,1)}) fusion(bf16[1,1024,1024]{1,2,0:T(8,128)(2,1)S(1)} %copy-done.1, bf16[1024,1024]{0,1:T(8,128)(2,1)} %fusion.38, bf16[1,1024,4096]{2,0,1:T(2,128)(2,1)} %all-gather.31.cloned.1.call-done, bf16[1024,4096]{1,0:T(8,128)(2,1)} %fusion.52, f32[1024,4096]{1,0:T(8,128)} %fusion.40), kind=kOutput, calls=%fused_computation.79 | convolution fusion | flops 8621390848 | bytes 39849984 | tf_op jit(solution)/vmap(transpose(jvp()))/dot_general | solution.py:21
  1036.0 17.4 fusion.16
  1053.4 23.8 fusion.96
  1077.2 21.4 fusion.20
  1098.7 23.8 fusion.101
  1122.4 531.6 %all-reduce.12 = (bf16[4096,1024]{0,1:T(8,128)(2,1)}, bf16[4096,1024]{0,1:T(8,128)(2,1)}, bf16[4096,1024]{0,1:T(8,128)(2,1)}, bf16[4096,1024]{0,1:T(8,128)(2,1)}) all-reduce(f32[4096,1024]{0,1:T(8,128)} %fusion.96, f32[4096,1024]{0,1:T(8,128)} %fusion.101, f32[4096,1024]{0,1:T(8,128)} %fusion.16, ...), channel_id=25, replica_groups=mesh['axis_0'=256] {'axis_0'}, use_global_device_ids=true, to_apply=%add.1.clone.clone | all-reduce | flops 16777216 | bytes 100663296
  1657.2 537.9 %reduce-scatter.13.cloned.1.call-done = f32[1024,16]{0,1:T(8,128)} async-done(((f32[1024,4096]{0,1:T(8,128)}), f32[1024,16]{0,1:T(8,128)}) %reduce-scatter.13.cloned.1.call-update) | async-done | bytes 65552
  2195.9 1302.7 %reduce-scatter.11.cloned.1.call-done = f32[16,1024]{1,0:T(8,128)} async-done(((f32[4096,1024]{1,0:T(8,128)}), f32[16,1024]{1,0:T(8,128)}) %reduce-scatter.11.cloned.1.call-update) | async-done | bytes 65552
  (67 shorter events, 78.0 us)
Async XLA Ops:
  7.2 134.3 %all-gather.29.cloned.1.call-start = ((), (), s32[]{:S(2)}) async-start(), calls=%async_computation.2 | async-start | bytes 16842752 | tf_op jit(solution)/vmap(jvp())/squeeze | solution.py:27
  8.7 259.4 %all-gather.31.cloned.1.call-start = ((), (), s32[]{:S(2)}) async-start(), calls=%async_computation.3 | async-start | bytes 16842752 | tf_op jit(solution)/vmap(jvp())/squeeze | solution.py:27
  10.3 376.8 %all-gather.33.cloned.1.call-start = ((), (), s32[]{:S(2)}) async-start(), calls=%async_computation.4 | async-start | bytes 8421376 | tf_op jit(solution)/vmap(jvp())/squeeze | solution.py:27
  11.8 501.5 %all-gather.35.cloned.1.call-start = ((), (), s32[]{:S(2)}) async-start(), calls=%async_computation.5 | async-start | bytes 16842752 | tf_op jit(solution)/vmap(jvp())/squeeze | solution.py:27
  12.5 619.6 %all-gather.37.cloned.1.call-start = ((), (), s32[]{:S(2)}) async-start(), calls=%async_computation.6 | async-start | bytes 8421376 | tf_op jit(solution)/vmap(jvp())/squeeze | solution.py:27
  13.1 744.6 %all-gather.39.cloned.1.call-start = ((), (), s32[]{:S(2)}) async-start(), calls=%async_computation.7 | async-start | bytes 16842752 | tf_op jit(solution)/vmap(jvp())/squeeze | solution.py:27
  13.8 2181.3 %reduce-scatter.13.cloned.1.call-start = ((), (), s32[]{:S(2)}) async-start(), calls=%async_computation.9 | async-start | bytes 16842752
  16.8 370.3 %copy-start = (bf16[1,1024,1024]{1,2,0:T(8,128)(2,1)}, bf16[1,1024,1024]{1,2,0:T(8,128)(2,1)S(1)}, u32[]{:S(2)}) copy-start(bf16[1,1024,1024]{1,2,0:T(8,128)(2,1)S(1)} %copy.15) | copy-start | bytes 6291460
  17.3 0.8 copy-start.5
  18.1 250.1 %copy-start.7 = (f32[1,1024]{1,0:T(1,128)}, f32[1,1024]{1,0:T(1,128)S(1)}, u32[]{:S(2)}) copy-start(f32[1,1024]{1,0:T(1,128)S(1)} %rsqrt.22) | copy-start | bytes 12292
  402.1 471.9 %copy-start.9 = (f32[1,1024]{1,0:T(1,128)}, f32[1,1024]{1,0:T(1,128)S(1)}, u32[]{:S(2)}) copy-start(f32[1,1024]{1,0:T(1,128)S(1)} %rsqrt.23) | copy-start | bytes 12292
  531.7 226.1 %copy-start.3 = (bf16[1,1024,1024]{1,2,0:T(8,128)(2,1)S(1)}, bf16[1,1024,1024]{1,2,0:T(8,128)(2,1)}, u32[]{:S(2)}) copy-start(bf16[1,1024,1024]{1,2,0:T(8,128)(2,1)} %get-tuple-element.23) | copy-start | bytes 6291460
  878.4 35.0 copy-start.2
  893.7 2604.9 %reduce-scatter.11.cloned.1.call-start = ((), (), s32[]{:S(2)}) async-start(), calls=%async_computation.8 | async-start | bytes 16842752
  927.9 51.0 %copy-start.1 = (bf16[1,1024,1024]{1,2,0:T(8,128)(2,1)S(1)}, bf16[1,1024,1024]{1,2,0:T(8,128)(2,1)}, u32[]{:S(2)}) copy-start(bf16[1,1024,1024]{1,2,0:T(8,128)(2,1)} %copy-done) | copy-start | bytes 6291460
  978.9 48.1 %copy-start.6 = (f32[1024]{0:T(1024)S(1)}, f32[1024]{0:T(1024)}, u32[]{:S(2)}) copy-start(f32[1024]{0:T(1024)} %copy-done.5) | copy-start | bytes 12292
  978.9 48.1 %copy-start.8 = (f32[1,1024]{1,0:T(1,128)S(1)}, f32[1,1024]{1,0:T(1,128)}, u32[]{:S(2)}) copy-start(f32[1,1024]{1,0:T(1,128)} %copy-done.7) | copy-start | bytes 12292
  1053.4 23.8 copy-start.10
  1077.2 21.4 copy-start.4
Sparse Core Ops, SparseCore 0:
  12.3 129.1 all-gather.28
  145.8 122.2 all-gather.30
  271.9 115.1 all-gather.32
  391.2 122.0 all-gather.34
  516.9 115.1 all-gather.36
  635.7 122.0 all-gather.38
  893.8 1301.2 reduce-scatter.12
  2197.6 1301.0 reduce-scatter.10
where the time goes:
time: 3520 us; the launch traced here: 3510 us
  waiting for transfers between devices  2480 us (70%)
  blocking collectives  532 us (15%)
  matrix products  434 us (12%)
    unnamed x10, waiting for transfers between devices  1840 us
    squeeze x6, waiting for transfers between devices, stack(): h = layer(h, {name: w[number] for name, w in weights.items()})  638 us
    unnamed x1, blocking collectives  532 us
    dot_general x6, matrix products, layer(): gate = jnp.dot(a, w['w_gate'], preferred_element_type=jnp.float32)  185 us
    dot_general x6, matrix products, layer(): up = jnp.dot(a, w['w_up'], preferred_element_type=jnp.float32)  170 us
    dot_general x5, matrix products, matmul(): jnp.dot(a, w, preferred_element_type=jnp.float32).astype(jnp.bfloat16)  79.2 us
  transfers between devices with their start and end apart: 8, of which 8 were waited for; matrix products, arithmetic and copies ran while one was open for 10% of the time, Pallas kernels for 0%

commit v1 on v0

v1 whole, which is shorter than its diff:
```python
import functools
import heapq

import jax
import jax.numpy as jnp
from jax import lax
from jax.experimental import pallas as pl
from jax.experimental.pallas import tpu as pltpu
from jax.sharding import PartitionSpec as P

F32, BF16 = jnp.float32, jnp.bfloat16
MESH = pl.DeviceIdType.MESH
AXES = ("x", "y", "z")
DIMS = {256: (4, 4, 8), 128: (4, 4, 4), 64: (4, 4, 2), 32: (4, 2, 2), 16: (2, 2, 2)}
ORDERS = (("x", "y", "z"), ("z", "y", "x"), ("z", "x", "y"))
EPS = 1e-6
VMEM_LIMIT = 63 * 1024 * 1024


class Place:
    def __init__(self, dims):
        self.dims = dict(zip(AXES, dims, strict=True))
        nx, ny, nz = dims
        me = lax.axis_index("dp")
        self.core = me % 2
        self.other = 1 - self.core
        self.partner = me + 1 - 2 * self.core
        self.at = {"x": me // (2 * nz * ny), "y": (me // (2 * nz)) % ny, "z": (me // 2) % nz}

    def along(self, axis, by):
        n = self.dims[axis]
        return (self.at[axis] + (by % n)) % n

    def neighbour(self, axis, by):
        at = dict(self.at)
        at[axis] = self.along(axis, by)
        return ((at["x"] * self.dims["y"] + at["y"]) * self.dims["z"] + at["z"]) * 2 + self.core

    def barrier(self):
        semaphore = pltpu.get_barrier_semaphore()
        peers = [self.neighbour(axis, by) for axis in AXES for by in (1, -1)] + [self.partner]
        for peer in peers:
            pl.semaphore_signal(semaphore, inc=1, device_id={"dp": peer}, device_id_type=MESH)
        pl.semaphore_wait(semaphore, len(peers))


def piece(ref, index, tall, half=None, sub=None):
    rows, columns = ref.shape[-2:]
    length = rows if tall else columns
    start = 0
    if half is not None:
        length //= 2
        start = half * length
    if sub is not None:
        length //= 2
        start = start + sub * length
    if half is None and sub is None:
        cut = slice(None)
    else:
        cut = pl.ds(pl.multiple_of(start, 8 if tall else 128) if half is not None else start, length)
    return ref.at[(*index, cut, slice(None))] if tall else ref.at[(*index, slice(None), cut)]


def messages(dims, order):
    dims = dict(zip(AXES, dims, strict=True))
    return [(k, s, d) for k, axis in enumerate(order) for s in range(1, dims[axis] // 2 + 1) for d in (0, 1)]


class Gather:
    def __init__(self, place, dims, which, buffer, send, receive, pass_send, pass_receive):
        self.place, self.order, self.tall = place, ORDERS[which], which == 2
        self.buffer, self.send, self.receive = buffer, send, receive
        self.pass_send, self.pass_receive = pass_send.at[which], pass_receive.at[which]
        self.ids = {m: i for i, m in enumerate(messages(dims, self.order))}

    def half_length(self, k):
        return self.place.dims[self.order[k]] // 2

    def region(self, k, s, d, behind):
        axis = self.order[k]
        by = -behind if d == 0 else behind
        index = [
            slice(None) if a in self.order[:k] else self.place.along(a, by if a == axis else 0) for a in AXES
        ]
        return piece(self.buffer, index, self.tall, self.place.core, None if s < self.half_length(k) else d)

    def ring(self, k, s, d):
        region = self.region(k, s, d, s - 1)
        i = self.ids[k, s, d]
        peer = self.place.neighbour(self.order[k], 1 if d == 0 else -1)
        return pltpu.make_async_remote_copy(
            region, region, self.send.at[i], self.receive.at[i], device_id={"dp": peer}, device_id_type=MESH
        )

    def pass_on(self, region):
        return pltpu.make_async_remote_copy(
            region, region, self.pass_send, self.pass_receive, device_id={"dp": self.place.partner}, device_id_type=MESH
        )

    def begin(self):
        self.ring(0, 1, 0).start()
        self.ring(0, 1, 1).start()
        index = [self.place.at[a] for a in AXES]
        self.pass_on(piece(self.buffer, index, self.tall, self.place.core)).start()

    def take(self, k, s, d):
        self.ring(k, s, d).wait_recv()
        if s < self.half_length(k):
            self.ring(k, s + 1, d).start()
        elif d == 1 and k < 2:
            self.ring(k + 1, 1, 0).start()
            self.ring(k + 1, 1, 1).start()
        self.pass_on(self.region(k, s, d, s)).start()

    def finish(self):
        blocks = [slice(None)] * 3
        self.pass_on(piece(self.buffer, blocks, self.tall, self.place.other)).wait_recv()

    def drain(self):
        for m in self.ids:
            self.ring(*m).wait_send()
        blocks = [slice(None)] * 3
        self.pass_on(piece(self.buffer, blocks, self.tall, self.place.core)).wait_send()


LINK, LATENCY = 46.6e3, 2.2


def gather_plan(dims, block_bytes, start=(0.0, 0.0, 0.0), grid=None):
    sizes = dict(zip(AXES, dims, strict=True))
    free, heap, out = {}, [], []

    def post(t, m, k, s, d):
        axis = ORDERS[m][k]
        blocks = 1
        for a in ORDERS[m][:k]:
            blocks *= sizes[a]
        size = block_bytes / 2 * blocks * (0.5 if s == sizes[axis] // 2 else 1)
        begin = max(t, free.get((axis, d), 0.0))
        free[axis, d] = begin + size / LINK
        heapq.heappush(heap, (begin + size / LINK + LATENCY, m, k, s, d))

    for m, t in enumerate(start):
        post(t, m, 0, 1, 0)
        post(t, m, 0, 1, 1)
    got = {}
    while heap:
        t, m, k, s, d = heapq.heappop(heap)
        if grid is not None:
            t = grid * -(-t // grid)
        got.setdefault((m, k, s), []).append(d)
        h = sizes[ORDERS[m][k]] // 2
        if s < h:
            out.append((t, m, (k, s, d)))
            post(t, m, k, s + 1, d)
        elif len(got[m, k, s]) == 2:
            out.append((t, m, (k, s, 0)))
            out.append((t, m, (k, s, 1)))
            if k < 2:
                post(t, m, k + 1, 1, 0)
                post(t, m, k + 1, 1, 1)
    return out


def gather_scratch(dims, sizes):
    depth, width = sizes
    wide = (*dims, 8, width)
    counts = [len(messages(dims, order)) for order in ORDERS]
    return [
        pltpu.VMEM(wide, BF16),
        pltpu.VMEM(wide, BF16),
        pltpu.VMEM((*dims, 32, depth), BF16),
        pltpu.VMEM((2, 4, width // 2), BF16),
        pltpu.VMEM((2, 8, width // 2), F32),
        *[pltpu.SemaphoreType.DMA((n,)) for n in counts],
        *[pltpu.SemaphoreType.DMA((n,)) for n in counts],
        pltpu.SemaphoreType.DMA((3,)),
        pltpu.SemaphoreType.DMA((3,)),
        pltpu.SemaphoreType.DMA((2,)),
        pltpu.SemaphoreType.DMA((2,)),
        pltpu.SemaphoreType.DMA((4,)),
    ]


class LayerGather:
    def __init__(self, dims, shards, outs, scratch):
        self.place = Place(dims)
        self.shards, self.outs = shards, outs
        self.buffers = scratch[:3]
        self.peer_rows, self.wide_rows = scratch[3:5]
        sends, receives = scratch[5:8], scratch[8:11]
        pass_send, pass_receive, self.swap_send, self.swap_receive, self.local = scratch[11:16]
        self.matrices = [
            Gather(self.place, dims, m, self.buffers[m], sends[m], receives[m], pass_send, pass_receive) for m in range(3)
        ]

    def halves(self, ref, core):
        width = ref.shape[-1] // 2
        return ref.at[:, pl.ds(pl.multiple_of(core * width, 128), width)]

    def swap(self, m):
        return pltpu.make_async_remote_copy(
            self.halves(self.shards[m], self.place.other),
            self.peer_rows.at[m],
            self.swap_send.at[m],
            self.swap_receive.at[m],
            device_id={"dp": self.place.partner},
            device_id_type=MESH,
        )

    def begin(self):
        place = self.place
        at = [place.at[a] for a in AXES]
        self.swap(0).start()
        self.swap(1).start()
        down = pltpu.make_async_copy(
            self.shards[2], piece(self.buffers[2], at, True, place.core), self.local.at[3]
        )
        down.start()
        down.wait()
        self.matrices[2].begin()
        for m in range(2):
            self.swap(m).wait_recv()
            mine = self.shards[m][:, pl.ds(pl.multiple_of(place.core * (self.shards[m].shape[1] // 2), 128), self.shards[m].shape[1] // 2)]
            theirs = self.peer_rows[m]

            @pl.when(place.core == 0)
            def _():
                self.wide_rows[m, 0:4] = mine.astype(F32)
                self.wide_rows[m, 4:8] = theirs.astype(F32)

            @pl.when(place.core == 1)
            def _():
                self.wide_rows[m, 0:4] = theirs.astype(F32)
                self.wide_rows[m, 4:8] = mine.astype(F32)

            width = self.shards[m].shape[1] // 2
            self.buffers[m][(*at, slice(None), pl.ds(pl.multiple_of(place.core * width, 128), width))] = self.wide_rows[
                m
            ].astype(BF16)
        for m in range(2):
            self.matrices[m].begin()

    def take(self, m, message):
        self.matrices[m].take(*message)

    def store(self, m):
        return pltpu.make_async_copy(self.buffers[m], self.outs[m], self.local.at[m])

    def finish(self):
        for m in range(3):
            self.matrices[m].finish()
            self.store(m).start()
        for m in range(2):
            self.swap(m).wait_send()
        for m in range(3):
            self.matrices[m].drain()
        for m in range(3):
            self.store(m).wait()


def gather_kernel(dims, plan, gate, up, down, gate_out, up_out, down_out, *scratch):
    work = LayerGather(dims, (gate, up, down), (gate_out, up_out, down_out), scratch)
    work.place.barrier()
    work.begin()
    for _, m, message in plan:
        work.take(m, message)
    work.finish()


def weights_shapes(dims, depth, width):
    return [
        jax.ShapeDtypeStruct((*dims, 8, width), BF16),
        jax.ShapeDtypeStruct((*dims, 8, width), BF16),
        jax.ShapeDtypeStruct((*dims, 32, depth), BF16),
    ]


def gather(dims, gate, up, down, collective_id):
    width, depth = gate.shape[1], down.shape[1]
    outs = pl.pallas_call(
        functools.partial(gather_kernel, dims, gather_plan(dims, 16 * width)),
        out_shape=weights_shapes(dims, depth, width),
        in_specs=[pl.BlockSpec(memory_space=pltpu.VMEM)] * 2 + [pl.BlockSpec(memory_space=pl.ANY)],
        out_specs=[pl.BlockSpec(memory_space=pl.ANY)] * 3,
        scratch_shapes=gather_scratch(dims, (depth, width)),
        compiler_params=pltpu.CompilerParams(
            collective_id=collective_id, has_side_effects=True, vmem_limit_bytes=VMEM_LIMIT
        ),
        name=f"gather_{collective_id}",
    )(gate, up, down)
    return [out.reshape(-1, out.shape[-1]) for out in outs]


class Scatter:
    def __init__(self, place, dims, which, grad, own, theirs, short, full, send, receive, load, swap_send, swap_receive):
        self.place, self.order, self.tall = place, ORDERS[which][::-1], which == 2
        self.grad, self.own, self.theirs, self.short, self.full = grad, own, theirs, short, full
        self.send, self.receive = send, receive
        self.load_sem, self.swap_send, self.swap_receive = load, swap_send, swap_receive
        self.ids = {m: i for i, m in enumerate(messages(dims, self.order))}

    def half_length(self, k):
        return self.place.dims[self.order[k]] // 2

    def chunks(self):
        h = self.half_length(0)
        return [h, *[by for s in range(h - 1, 0, -1) for by in (s, -s)], 0]

    def chunk_index(self, by):
        return [self.place.along(a, by) if a == self.order[0] else slice(None) for a in AXES]

    def load(self, i):
        index = self.chunk_index(self.chunks()[i])
        return pltpu.make_async_copy(
            piece(self.grad, index, self.tall, self.place.core), self.own.at[tuple(index)], self.load_sem.at[i]
        )

    def swap(self, i):
        index = self.chunk_index(self.chunks()[i])
        return pltpu.make_async_remote_copy(
            piece(self.grad, index, self.tall, self.place.other),
            self.theirs.at[tuple(index)],
            self.swap_send.at[i],
            self.swap_receive.at[i],
            device_id={"dp": self.place.partner},
            device_id_type=MESH,
        )

    def begin(self, i):
        self.swap(i).start()
        self.load(i).start()

    def ready(self, i):
        self.load(i).wait()
        self.swap(i).wait_recv()

    def index(self, k, by):
        return [
            slice(None) if a in self.order[k + 1 :] else self.place.along(a, by if self.order[k : k + 1] == (a,) else 0)
            for a in AXES
        ]

    def ring(self, k, s, d):
        h = self.half_length(k)
        by = h - s + 1 if d == 0 else -(h - s + 1)
        source = piece(self.own, self.index(k, by), self.tall, sub=d if s == 1 else None)
        landing = self.short[k].at[d] if s == 1 else self.full[k].at[d, s - 2]
        i = self.ids[k, s, d]
        peer = self.place.neighbour(self.order[k], 1 if d == 0 else -1)
        return pltpu.make_async_remote_copy(
            source, landing, self.send.at[i], self.receive.at[i], device_id={"dp": peer}, device_id_type=MESH
        )

    def terms(self, k, index):
        whole, quarters = [self.own.at[tuple(index)], self.theirs.at[tuple(index)]], ([], [])
        for j in range(k):
            at = [index[AXES.index(a)] for a in AXES if a in self.order[j + 1 :]]
            h = self.half_length(j)
            for d in (0, 1):
                if h == 1:
                    quarters[d].append(self.short[j].at[(d, *at)])
                else:
                    whole.append(self.full[j].at[(d, h - 2, *at)])
        return whole, quarters

    def add(self, k, by, arrived=None, out=None):
        free = [a for a in AXES if a in self.order[k + 1 :]]
        sizes = [self.place.dims[a] for a in free]
        count = 1
        for n in sizes:
            count *= n
        fixed = self.index(k, by)

        def one(i):
            at, rest = {}, i
            for a, n in reversed(list(zip(free, sizes, strict=True))):
                at[a], rest = (rest % n, rest // n) if a != free[0] else (rest, 0)
            index = [at[a] if a in free else fixed[j] for j, a in enumerate(AXES)]
            whole, quarters = self.terms(k, index)
            whole, quarters = list(whole), (list(quarters[0]), list(quarters[1]))
            place = [at[a] for a in free]
            if arrived is not None:
                s, d = arrived
                if s == 1:
                    quarters[d].append(self.short[k].at[(d, *place)])
                else:
                    whole.append(self.full[k].at[(d, s - 2, *place)])
            target = self.own.at[tuple(index)] if out is None else out
            for q in (0, 1):
                length = target.shape[0 if self.tall else 1] // 2
                cut = (slice(q * length, (q + 1) * length), slice(None))
                cut = cut if self.tall else cut[::-1]
                total = None
                for ref in whole:
                    value = ref[cut].astype(F32)
                    total = value if total is None else total + value
                for ref in quarters[q]:
                    total = total + ref[...].astype(F32)
                target[cut] = total.astype(BF16)

        if count == 1:
            one(0)
        else:
            pl.loop(0, count)(one)

    def first(self, k):
        h = self.half_length(k)
        if k == 0:
            self.ready(0)
        self.add(k, h)
        self.ring(k, 1, 0).start()
        self.ring(k, 1, 1).start()

    def take(self, k, s, d):
        h = self.half_length(k)
        self.ring(k, s, d).wait_recv()
        if s < h:
            by = h - s if d == 0 else -(h - s)
            if k == 0:
                self.ready(self.chunks().index(by))
            self.add(k, by, (s, d))
            self.ring(k, s + 1, d).start()
        elif d == 1:
            if k == 0:
                self.ready(len(self.chunks()) - 1)
            if k < 2:
                self.first(k + 1)

    def result(self, out):
        self.add(3, 0, out=out)

    def drain(self):
        for m in self.ids:
            self.ring(*m).wait_send()
        for i in range(len(self.chunks())):
            self.swap(i).wait_send()


D2D, HBM, ADD = 500e3, 3000e3, 250e3


def scatter_plan(dims, block_bytes, grid=None):
    sizes = dict(zip(AXES, dims, strict=True))
    chips = dims[0] * dims[1] * dims[2]
    orders = [order[::-1] for order in ORDERS]
    free, heap, out = {}, [], []
    swapped, swap_time = {}, LATENCY + 1.0
    hs = [[sizes[a] // 2 for a in order] for order in orders]
    lists = [[h[0], *[by for s in range(h[0] - 1, 0, -1) for by in (s, -s)], 0] for h in hs]
    queue = sorted(((i + 1) / len(c), m, by) for m, c in enumerate(lists) for i, by in enumerate(c))
    for _, m, by in queue:
        swap_time += block_bytes / 2 * chips / sizes[orders[m][0]] / D2D
        swapped[m, by] = swap_time

    def size_of(m, k):
        blocks = 1
        for a in orders[m][k + 1 :]:
            blocks *= sizes[a]
        return block_bytes / 2 * blocks

    def post(t, m, k, s, d):
        size = size_of(m, k) * (0.5 if s == 1 else 1)
        begin = max(t, free.get((orders[m][k], d), 0.0))
        free[orders[m][k], d] = begin + size / LINK
        ready = begin + size / LINK + LATENCY
        h = hs[m][k]
        if k == 0 and s <= h:
            by = (h - s) * (1 if d == 0 else -1)
            ready = max(ready, swapped[m, by if s < h else 0])
        heapq.heappush(heap, (ready, m, k, s, d))

    clock = 0.0
    for m in range(3):
        heapq.heappush(heap, (swapped[m, hs[m][0]], m, -1, 0, 0))
    got = {}
    while heap:
        ready, m, k, s, d = heapq.heappop(heap)
        t = max(ready, clock)
        if grid is not None:
            t = max(clock, grid * -(-ready // grid))
        if k < 0:
            clock = t + size_of(m, 0) / ADD
            out.append((t, m, None))
            post(clock, m, 0, 1, 0)
            post(clock, m, 0, 1, 1)
            continue
        h = hs[m][k]
        if s < h:
            clock = t + size_of(m, k) / ADD
            out.append((t, m, (k, s, d)))
            post(clock, m, k, s + 1, d)
            continue
        got.setdefault((m, k), []).append(d)
        if len(got[m, k]) == 2:
            out.append((t, m, (k, s, 0)))
            out.append((t, m, (k, s, 1)))
            if k < 2:
                clock = t + size_of(m, k + 1) / ADD
                post(clock, m, k + 1, 1, 0)
                post(clock, m, k + 1, 1, 1)
    return out, [(m, lists[m].index(by)) for _, m, by in queue]


def scatter_scratch(dims, depth, width):
    sizes = dict(zip(AXES, dims, strict=True))
    out = []
    for m, order in enumerate(ORDERS):
        order = order[::-1]
        block = (16, depth) if m == 2 else (8, width // 2)
        short = (8, depth) if m == 2 else (8, width // 4)
        out += [pltpu.VMEM((*dims, *block), BF16)] * 2
        for k, axis in enumerate(order):
            rest = [sizes[a] for a in AXES if a in order[k + 1 :]]
            h = sizes[axis] // 2
            out.append(pltpu.VMEM((2, *rest, *short), BF16))
            if h > 1:
                out.append(pltpu.VMEM((2, h - 1, *rest, *block), BF16))
        n, c = len(messages(dims, order)), sizes[order[0]]
        out += [pltpu.SemaphoreType.DMA((n,))] * 2 + [pltpu.SemaphoreType.DMA((c,))] * 3
    out += [pltpu.VMEM((2, 8, width // 2), BF16), pltpu.VMEM((2, 8, width // 2), BF16)]
    out += [pltpu.SemaphoreType.DMA((2,))] * 2 + [pltpu.SemaphoreType.DMA((1,)), pltpu.VMEM((16, depth), BF16)]
    return out


class LayerScatter:
    def __init__(self, dims, grads, outs, scratch):
        self.place, self.outs = Place(dims), outs
        scratch = list(scratch)
        self.matrices = []
        for m in range(3):
            own, theirs = scratch.pop(0), scratch.pop(0)
            short, full = [], []
            for axis in ORDERS[m][::-1]:
                short.append(scratch.pop(0))
                full.append(scratch.pop(0) if self.place.dims[axis] > 2 else None)
            semaphores = [scratch.pop(0) for _ in range(5)]
            self.matrices.append(Scatter(self.place, dims, m, grads[m], own, theirs, short, full, *semaphores))
        self.mine, self.peer, self.send, self.receive, self.local, self.down = scratch

    def begin(self, loads):
        for m, i in loads:
            self.matrices[m].begin(i)

    def take(self, m, message):
        if message is None:
            self.matrices[m].first(0)
        else:
            self.matrices[m].take(*message)

    def swap(self, m):
        return pltpu.make_async_remote_copy(
            self.mine.at[m],
            self.peer.at[m],
            self.send.at[m],
            self.receive.at[m],
            device_id={"dp": self.place.partner},
            device_id_type=MESH,
        )

    def finish(self):
        for m in range(2):
            self.matrices[m].result(self.mine.at[m])
        self.matrices[2].result(self.outs[2])
        for m in range(2):
            self.swap(m).start()
        for m in range(3):
            self.matrices[m].drain()
        for m in range(2):
            self.swap(m).wait_recv()
            mine, peer = self.mine[m].astype(F32), self.peer[m].astype(F32)
            width = mine.shape[1]

            @pl.when(self.place.core == 0)
            def _():
                self.outs[m][:, :width] = mine[0:4].astype(BF16)
                self.outs[m][:, width:] = peer[0:4].astype(BF16)

            @pl.when(self.place.core == 1)
            def _():
                self.outs[m][:, :width] = peer[4:8].astype(BF16)
                self.outs[m][:, width:] = mine[4:8].astype(BF16)

        for m in range(2):
            self.swap(m).wait_send()


def scatter_kernel(dims, plan, loads, gate, up, down, gate_out, up_out, down_out, *scratch):
    work = LayerScatter(dims, (gate, up, down), (gate_out, up_out, down_out), scratch)
    work.place.barrier()
    work.begin(loads)
    for _, m, message in plan:
        work.take(m, message)
    work.finish()


def scatter(dims, grads, collective_id):
    width, depth = grads[0].shape[1], grads[2].shape[1]
    shapes = weights_shapes(dims, depth, width)
    plan, loads = scatter_plan(dims, 16 * width)
    return pl.pallas_call(
        functools.partial(scatter_kernel, dims, plan, loads),
        out_shape=[
            jax.ShapeDtypeStruct((4, width), BF16),
            jax.ShapeDtypeStruct((4, width), BF16),
            jax.ShapeDtypeStruct((16, depth), BF16),
        ],
        in_specs=[pl.BlockSpec(memory_space=pl.ANY)] * 3,
        out_specs=[pl.BlockSpec(memory_space=pltpu.VMEM)] * 3,
        scratch_shapes=scatter_scratch(dims, depth, width),
        compiler_params=pltpu.CompilerParams(
            collective_id=collective_id, has_side_effects=True, vmem_limit_bytes=VMEM_LIMIT
        ),
        name=f"scatter_{collective_id}",
    )(*[g.reshape(s.shape) for g, s in zip(grads, shapes, strict=True)])


def dot(a, b, ca, cb):
    return lax.dot_general(a, b, (((ca,), (cb,)), ((), ())), preferred_element_type=F32)


def normed(h):
    wide = h.astype(F32)
    return (wide * lax.rsqrt(jnp.mean(wide * wide, -1, keepdims=True) + EPS)).astype(BF16)


def forward_kernel(h, gate, up, down, a_out, h_out, next_out, total):
    j, last = pl.program_id(0), pl.num_programs(0) - 1

    @pl.when(j == 0)
    def _():
        a_out[...] = normed(h[...])
        total[...] = jnp.zeros_like(total)

    a = a_out[...]
    g = dot(a, gate[...], 1, 0)
    u = dot(a, up[...], 1, 0)
    p = (g * jax.nn.sigmoid(g) * u).astype(BF16)
    total[...] += dot(p, down[...], 1, 0)

    @pl.when(j == last)
    def _():
        out = (h[...].astype(F32) + total[...].astype(BF16).astype(F32)).astype(BF16)
        h_out[...] = out
        next_out[...] = normed(out)


def forward(h, gate, up, down, tile=512):
    tokens, depth = h.shape
    tile = min(tile, gate.shape[1])
    whole = pl.BlockSpec((tokens, depth), lambda j: (0, 0))
    wide = pl.BlockSpec((depth, tile), lambda j: (0, j))
    tall = pl.BlockSpec((tile, depth), lambda j: (j, 0))
    return pl.pallas_call(
        forward_kernel,
        grid=(gate.shape[1] // tile,),
        out_shape=[jax.ShapeDtypeStruct((tokens, depth), BF16)] * 3,
        in_specs=[whole, wide, wide, tall],
        out_specs=[whole] * 3,
        scratch_shapes=[pltpu.VMEM((tokens, depth), F32)],
        compiler_params=pltpu.CompilerParams(vmem_limit_bytes=VMEM_LIMIT),
        cost_estimate=pl.CostEstimate(
            flops=6 * tokens * depth * gate.shape[1], bytes_accessed=6 * gate.size + 8 * h.size, transcendentals=0
        ),
        name="forward",
    )(h, gate, up, down)


def backward_kernel(a, h, dh, gate, up, down, dgate_out, dup_out, ddown_out, dh_out, total):
    j, last = pl.program_id(0), pl.num_programs(0) - 1

    @pl.when(j == 0)
    def _():
        total[...] = jnp.zeros_like(total)

    a_, dh_ = a[...], dh[...]
    gate_, up_ = gate[...], up[...]
    g = dot(a_, gate_, 1, 0)
    u = dot(a_, up_, 1, 0)
    s = jax.nn.sigmoid(g)
    silu = g * s
    ddown_out[...] = dot((silu * u).astype(BF16), dh_, 0, 0).astype(BF16)
    dp = dot(dh_, down[...], 1, 1).astype(BF16).astype(F32)
    du = (dp * silu).astype(BF16)
    dg = (dp * u * (s + silu * (1 - s))).astype(BF16)
    dgate_out[...] = dot(a_, dg, 0, 0).astype(BF16)
    dup_out[...] = dot(a_, du, 0, 0).astype(BF16)
    total[...] += dot(dg, gate_, 1, 1) + dot(du, up_, 1, 1)

    @pl.when(j == last)
    def _():
        wide = h[...].astype(F32)
        scale = lax.rsqrt(jnp.mean(wide * wide, -1, keepdims=True) + EPS)
        da = total[...].astype(BF16).astype(F32)
        along = jnp.mean(da * wide, -1, keepdims=True)
        dwide = scale * (da - wide * (scale * scale * along))
        dh_out[...] = (dh[...].astype(F32) + dwide.astype(BF16).astype(F32)).astype(BF16)


def backward(a, h, dh, gate, up, down, tile=512):
    tokens, depth = h.shape
    tile = min(tile, gate.shape[1])
    whole = pl.BlockSpec((tokens, depth), lambda j: (0, 0))
    wide = pl.BlockSpec((depth, tile), lambda j: (0, j))
    tall = pl.BlockSpec((tile, depth), lambda j: (j, 0))
    return pl.pallas_call(
        backward_kernel,
        grid=(gate.shape[1] // tile,),
        out_shape=[
            jax.ShapeDtypeStruct(gate.shape, BF16),
            jax.ShapeDtypeStruct(gate.shape, BF16),
            jax.ShapeDtypeStruct(down.shape, BF16),
            jax.ShapeDtypeStruct((tokens, depth), BF16),
        ],
        in_specs=[whole, whole, whole, wide, wide, tall],
        out_specs=[wide, wide, tall, whole],
        scratch_shapes=[pltpu.VMEM((tokens, depth), F32)],
        compiler_params=pltpu.CompilerParams(vmem_limit_bytes=VMEM_LIMIT),
        cost_estimate=pl.CostEstimate(
            flops=16 * tokens * depth * gate.shape[1], bytes_accessed=12 * gate.size + 8 * h.size, transcendentals=0
        ),
        name="backward",
    )(a, h, dh, gate, up, down)


def solution(mesh):
    dims = DIMS[mesh.shape["dp"]]

    def local(x, dy, w_gate, w_up, w_down):
        h, dh = x[0], dy[0]
        first = gather(dims, w_gate[0], w_up[0], w_down[0], 1)
        second = gather(dims, w_gate[1], w_up[1], w_down[1], 2)
        a1, h1, a2 = forward(h, *first)
        *grads2, dh1 = backward(a2, h1, dh, *second)
        sums2 = scatter(dims, grads2, 3)
        *grads1, dh0 = backward(a1, h, dh1, *first)
        sums1 = scatter(dims, grads1, 4)
        return (dh0[None], *(jnp.stack(both) for both in zip(sums1, sums2, strict=True)))

    rows = P(None, "dp", None)
    return jax.shard_map(
        local,
        mesh=mesh,
        in_specs=(P(("rep", "dp"), None, None),) * 2 + (rows,) * 3,
        out_specs=(P(("rep", "dp"), None, None),) + (P("rep", "dp", None),) * 3,
        check_vma=False,
    )
```

time: 3520 us -> 528 us (0.15)
  waiting for transfers between devices: 2480 us -> 0 us
  blocking collectives: 532 us -> 0 us
  Pallas kernels: 0 us -> 519 us
  matrix products: 434 us -> 0 us
    unnamed x10 -> x0, waiting for transfers between devices: 1840 us -> none
    squeeze x6 -> x0, waiting for transfers between devices: 638 us -> none  [stack(): h = layer(h, {name: w[number] for name, w in weights.items()})]
    unnamed x1 -> x0, blocking collectives: 532 us -> none
    pallas_call x0 -> x7, Pallas kernels: none -> 519 us  [the longest x2 169 us: backward(): pl.pallas_call(backward_kernel, grid=(gate.shape[1] // tile,), out_shape=...]
    dot_general x17 -> x0, matrix products: 434 us -> none  [the longest x6 185 us: layer(): gate = jnp.dot(a, w['w_gate'], preferred_element_type=jnp.float32)]
  transfers between devices with their start and end apart: 8 -> 0, of which waited for: 8 -> 0; matrix products, arithmetic and copies ran while one was open for 10% -> 0% of each run, Pallas kernels for 0% -> 0%
where the time goes in v1:
time: 528 us; the launch traced here: 527 us
  Pallas kernels  519 us (98%)
    pallas_call x2, Pallas kernels, backward(): pl.pallas_call(backward_kernel, grid=(gate.shape[1] // tile,), out_shape=...  169 us
    pallas_call x2, Pallas kernels, scatter(): pl.pallas_call(functools.partial(scatter_kernel, dims, plan, loads), out_...  164 us
    pallas_call x2, Pallas kernels, gather(): pl.pallas_call(functools.partial(gather_kernel, dims, gather_plan(dims, 1...  151 us
    pallas_call x1, Pallas kernels, forward(): pl.pallas_call(forward_kernel, grid=(gate.shape[1] // tile,), out_shape=[...  35.3 us

profile of v1, /device:TPU:1, one launch (start us, length us, event | category | flops | bytes accessed | tf_op | source)
XLA Modules:
  0.0 527.1 jit_solution(13984875159083412566)
XLA Ops:
  0.6 1.4 slice_bitcast_fusion
  2.0 1.5 slice_bitcast_fusion.1
  3.5 78.8 %gather_2.1 = (bf16[4,4,8,8,4096]{4,3,2,1,0:T(8,128)(2,1)}, bf16[4,4,8,8,4096]{4,3,2,1,0:T(8,128)(2,1)}, bf16[4,4,8,32,1024]{4,3,2,1,0:T(8,128)(2,1)}) custom-call(bf16[4,4096]{1,0:T(4,128)(2,1)} %get-tuple-element.57.gate, bf16[4,4096]{1,0:T(4,128)(2,1)} %get-tuple-element.52.up, bf16[16,1024]{1,0:T(8,128)(2,1)} %get-tuple-element.50.down), custom_call_target="tpu_custom_call" | custom-call | tf_op jit(solution)/shard_map/gather_2/pallas_call | solution.py:281
  82.4 72.0 %gather_1.1 = (bf16[4,4,8,8,4096]{4,3,2,1,0:T(8,128)(2,1)}, bf16[4,4,8,8,4096]{4,3,2,1,0:T(8,128)(2,1)}, bf16[4,4,8,32,1024]{4,3,2,1,0:T(8,128)(2,1)}) custom-call(bf16[4,4096]{1,0:T(4,128)(2,1)} %get-tuple-element.56.gate, bf16[4,4096]{1,0:T(4,128)(2,1)} %get-tuple-element.53.up, bf16[16,1024]{1,0:T(8,128)(2,1)} %get-tuple-element.51.down), custom_call_target="tpu_custom_call" | custom-call | tf_op jit(solution)/shard_map/gather_1/pallas_call | solution.py:281
  154.4 35.3 %forward.1 = (bf16[1024,1024]{1,0:T(8,128)(2,1)}, bf16[1024,1024]{1,0:T(8,128)(2,1)}, bf16[1024,1024]{1,0:T(8,128)(2,1)}) custom-call(bf16[1024,1024]{1,0:T(8,128)(2,1)} %bitcast.55, bf16[1024,4096]{1,0:T(8,128)(2,1)} %bitcast.45, bf16[1024,4096]{1,0:T(8,128)(2,1)} %bitcast.47, bf16[4096,1024]{1,0:T(8,128)(2,1)} %bitcast.49), custom_call_target="tpu_custom_call" | custom-call | flops 25769803776 | bytes 33554432 | tf_op jit(solution)/shard_map/forward/pallas_call | solution.py:654
  189.7 84.5 %backward.2 = (bf16[1024,4096]{1,0:T(8,128)(2,1)}, bf16[1024,4096]{1,0:T(8,128)(2,1)}, bf16[4096,1024]{1,0:T(8,128)(2,1)}, bf16[1024,1024]{1,0:T(8,128)(2,1)}) custom-call(bf16[1024,1024]{1,0:T(8,128)(2,1)} %get-tuple-element.31.a, bf16[1024,1024]{1,0:T(8,128)(2,1)} %get-tuple-element.32.h, bf16[1024,1024]{1,0:T(8,128)(2,1)} %bitcast.54, ...), custom_call_target="tpu_custom_call" | custom-call | flops 68719476736 | bytes 58720256 | tf_op jit(solution)/shard_map/backward/pallas_call | solution.py:706
  274.2 84.5 %backward.3 = (bf16[1024,4096]{1,0:T(8,128)(2,1)}, bf16[1024,4096]{1,0:T(8,128)(2,1)}, bf16[4096,1024]{1,0:T(8,128)(2,1)}, bf16[1024,1024]{1,0:T(8,128)(2,1)}) custom-call(bf16[1024,1024]{1,0:T(8,128)(2,1)} %get-tuple-element.30.a, bf16[1024,1024]{1,0:T(8,128)(2,1)} %bitcast.56, bf16[1024,1024]{1,0:T(8,128)(2,1)} %get-tuple-element.36.dh, ...), custom_call_target="tpu_custom_call" | custom-call | flops 68719476736 | bytes 58720256 | tf_op jit(solution)/shard_map/backward/pallas_call | solution.py:706
  358.7 82.5 %scatter_4.1 = (bf16[4,4096]{1,0:T(4,128)(2,1)}, bf16[4,4096]{1,0:T(4,128)(2,1)}, bf16[16,1024]{1,0:T(8,128)(2,1)}) custom-call(bf16[4,4,8,8,4096]{4,3,2,1,0:T(8,128)(2,1)} %bitcast.36, bf16[4,4,8,8,4096]{4,3,2,1,0:T(8,128)(2,1)} %bitcast.37, bf16[4,4,8,32,1024]{4,3,2,1,0:T(8,128)(2,1)} %bitcast.38), custom_call_target="tpu_custom_call" | custom-call | tf_op jit(solution)/shard_map/scatter_4/pallas_call | solution.py:601
  441.2 0.0 copy-start.2
  441.2 0.0 copy-start.1
  441.2 0.0 copy-start
  441.2 81.6 %scatter_3.1 = (bf16[4,4096]{1,0:T(4,128)(2,1)}, bf16[4,4096]{1,0:T(4,128)(2,1)}, bf16[16,1024]{1,0:T(8,128)(2,1)}) custom-call(bf16[4,4,8,8,4096]{4,3,2,1,0:T(8,128)(2,1)} %bitcast.33, bf16[4,4,8,8,4096]{4,3,2,1,0:T(8,128)(2,1)} %bitcast.34, bf16[4,4,8,32,1024]{4,3,2,1,0:T(8,128)(2,1)} %bitcast.35), custom_call_target="tpu_custom_call" | custom-call | tf_op jit(solution)/shard_map/scatter_3/pallas_call | solution.py:601
  522.9 0.0 copy-done.2
  522.9 1.4 pad_maximum_fusion
  524.3 0.0 copy-done.1
  524.3 1.4 pad_maximum_fusion.1
  525.7 0.0 copy-done
  525.7 1.4 pad_maximum_fusion.2
Async XLA Ops:
  441.2 81.7 %copy-start.2 = (bf16[4,4096]{1,0:T(4,128)(2,1)S(1)}, bf16[4,4096]{1,0:T(4,128)(2,1)}, u32[]{:S(2)}) copy-start(bf16[4,4096]{1,0:T(4,128)(2,1)} %get-tuple-element.41) | copy-start | bytes 98308
  441.2 83.1 %copy-start.1 = (bf16[4,4096]{1,0:T(4,128)(2,1)S(1)}, bf16[4,4096]{1,0:T(4,128)(2,1)}, u32[]{:S(2)}) copy-start(bf16[4,4096]{1,0:T(4,128)(2,1)} %get-tuple-element.46) | copy-start | bytes 98308
  441.2 84.5 %copy-start = (bf16[16,1024]{1,0:T(8,128)(2,1)S(1)}, bf16[16,1024]{1,0:T(8,128)(2,1)}, u32[]{:S(2)}) copy-start(bf16[16,1024]{1,0:T(8,128)(2,1)} %get-tuple-element.48) | copy-start | bytes 98308
